TPU v7x, 256 devices: a whole 4x4x8 slice. The times are simulated.
256 devices in a mesh: ep: 32 (over x, z), tp: 8 (over y, core).
Axes of the slice: x: 4, y: 4, z: 8, core: 2. Of those that a mesh axis runs over, the one named last changes fastest.
Arguments:
- tokens: bfloat16 [8192, 2880], P('ep', 'tp'), may hold values from -6 to 6
- expert_ids: int32 [8192, 4], P('ep'), may hold values from 0 to 63, all different within a row; in each aligned block of 256 rows (0 to 255, 256 to 511, ...) at most 32 rows name the same one
- combine_weights: float32 [8192, 4], P('ep'), may hold values from 0.05 to 0.6
- gate_weight: bfloat16 [64, 2880, 2880], P('ep', None, 'tp'), may hold values from -0.109375 to 0.109375
- up_weight: bfloat16 [64, 2880, 2880], P('ep', None, 'tp'), may hold values from -0.109375 to 0.109375
- down_weight: bfloat16 [64, 2880, 2880], P('ep', 'tp'), may hold values from -0.109375 to 0.109375
Outputs:
- mixed: bfloat16 [8192, 2880], P('ep', 'tp')
Inputs may be any that keep to these rules, and one draw needn't show every extreme that they name: `expert_ids`: each row names 4 different experts; within the 256 rows of one index of ep no expert is named more than 32 times, a bound that some block reaches.
All inputs are finite; a program needn't handle non-finite values.
Results may differ from a plain program's by a relative error of at most 0.014.
Values may be sent and summed in bfloat16 or wider, within the bound.
No kernel may reach another device: no remote copies, remote signals or barrier semaphores. Data moves between devices by JAX's collectives and lax.ppermute only.
A program may use at most 128 MiB of HBM per device.

v0:
```python
import jax
import jax.numpy as jnp
from jax import lax
from jax.sharding import Mesh
from jax.sharding import PartitionSpec as P

TP = ("tp_0", "tp_1")


def reduced_to_own(pieces, axes, sequence):
    inside = pieces.shape[1:]
    pieces = pieces.reshape(*(lax.axis_size(a) for a in axes), *inside)
    pieces = jnp.moveaxis(pieces, sequence, range(len(axes))).reshape(-1, *inside)
    for k in sequence:
        pieces = lax.psum_scatter(pieces, axes[k], scatter_dimension=0, tiled=True)
    return pieces[0]


def split_up(array, dim, count):
    before, after = (array.shape[:dim], array.shape[dim + 1 :])
    return jnp.moveaxis(array.reshape(*before, count, -1, *after), dim, 0)


def scatter_axes(array, axes, sequence, dim):
    count = lax.axis_size(axes)
    return reduced_to_own(split_up(array, dim, count), axes, sequence)


def activate(gate_acc, up_acc):
    return (up_acc + 1.0) * gate_acc * jax.nn.sigmoid(1.702 * gate_acc)


def local(tokens, expert_ids, combine_weights, gate_weight, up_weight, down_weight):
    ep_count = lax.axis_size("ep")
    exp_local = gate_weight.shape[0]
    experts = exp_local * ep_count
    tok_rows = expert_ids.shape[0]
    top_count = expert_ids.shape[1]
    capacity = 2 * tok_rows * top_count // experts
    feat_width = tokens.shape[1]
    flat_ids = expert_ids.reshape(-1)
    onehot = (flat_ids[:, None] == jnp.arange(experts, dtype=jnp.int32)[None, :]).astype(jnp.int32)
    slot_pos = jnp.sum((jnp.cumsum(onehot, axis=0) - onehot) * onehot, axis=1)
    expert_local = flat_ids % exp_local
    owner_dev = flat_ids // exp_local
    token_of = jnp.arange(tok_rows * top_count, dtype=jnp.int32) // top_count
    send_buf = jnp.zeros((exp_local, ep_count, capacity, feat_width), jnp.bfloat16)
    send_buf = send_buf.at[expert_local, owner_dev, slot_pos].set(tokens[token_of])
    arrived = lax.all_to_all(send_buf, "ep", split_axis=1, concat_axis=1, tiled=True)
    arrived = arrived.reshape(exp_local, ep_count * capacity, feat_width)
    shard_piece = lax.all_gather(arrived, TP, axis=2, tiled=True)
    gate_new = jnp.einsum(
        "erd,edf->erf", shard_piece, gate_weight, preferred_element_type=jnp.float32
    )
    up_new = jnp.einsum("erd,edf->erf", shard_piece, up_weight, preferred_element_type=jnp.float32)
    hidden = activate(gate_new, up_new).astype(jnp.bfloat16)
    partials = jnp.einsum("erf,efd->erd", hidden, down_weight, preferred_element_type=jnp.float32)
    weights_flat = combine_weights.reshape(-1)
    summed = scatter_axes(partials.astype(jnp.bfloat16), TP, (1, 0), 2).astype(jnp.float32)
    summed = summed.reshape(exp_local, ep_count, capacity, summed.shape[2])
    returned = lax.all_to_all(
        summed.astype(jnp.bfloat16), "ep", split_axis=1, concat_axis=1, tiled=True
    ).astype(summed.dtype)
    picked = returned[expert_local, owner_dev, slot_pos]
    weighted = (picked * weights_flat[:, None]).reshape(tok_rows, top_count, picked.shape[1])
    mixed = jnp.sum(weighted, axis=1).astype(jnp.bfloat16)
    return mixed


def solution(mesh):
    split = Mesh(mesh.devices.reshape(mesh.shape["ep"], 4, 2), ("ep", "tp_0", "tp_1"))
    placed = (
        P("ep", TP),
        P("ep", None),
        P("ep", None),
        P("ep", None, TP),
        P("ep", None, TP),
        P("ep", TP, None),
    )
    return jax.shard_map(local, mesh=split, in_specs=placed, out_specs=P("ep", TP), check_vma=False)
```

profile of v0, /device:TPU:32, one launch (start us, length us, event | category | flops | bytes accessed | tf_op | source)
XLA Modules:
  0.0 360.9 jit_solution(3638396333141942187)
XLA Ops:
  6.5 0.9 copy.61
  7.4 0.1 eq.31
  7.5 0.1 eq.27
  7.6 0.1 reshape.218
  7.8 18.0 %reduce-window.6 = s32[64,8,128]{2,1,0:T(8,128)S(1)} reduce-window(s32[64,8,128]{2,1,0:T(8,128)S(1)} %fusion.6, s32[]{:T(128)} %constant.47.clone.1), window={size=1x1x128 pad=0_0x0_0x127_0}, to_apply=%region_0.0 | reduce-window | flops 8323072 | bytes 524292 | tf_op jit(solution)/shard_map/reduce-window
  25.8 0.1 slice.13
  26.0 0.1 copy.64
  26.2 0.1 broadcast_add_fusion
  26.6 0.1 and_reduce_fusion
  26.7 0.2 copy.66
  26.9 9.4 %scatter_custom_fusion = bf16[2048,360]{1,0:T(8,128)(2,1)S(1)} fusion(s32[1024]{0:T(1024)S(1)} %get-tuple-element.10, bf16[256,360]{1,0:T(8,128)(2,1)S(1)} %copy.66, s32[1024]{0:T(1024)S(1)} %get-tuple-element.9, bf16[]{:T(256)} %constant.46.clone.1), kind=kCustom, calls=%fused_computation.7 | custom fusion | bytes 1474562
  36.3 0.3 copy.67
  36.6 51.1 %all_to_all.10 = bf16[2,32,32,360]{3,2,0,1:T(8,128)(2,1)S(1)} all-to-all(bf16[2,32,32,360]{3,2,0,1:T(8,128)(2,1)S(1)} %copy.67), channel_id=1, replica_groups=mesh['ep'=32,'tp_0'=4,'tp_1'=2] {'ep'}, dimensions={1} | all-to-all | bytes 2949120 | tf_op jit(solution)/shard_map/all_to_all | solution.py:49
  87.6 0.2 copy.68
  87.8 1.6 copy.69
  89.5 0.2 reduce-scatter.3.cloned.1.call-start
  89.7 62.7 %all-gather.2.cloned.1.call-done = bf16[2,1024,2880]{1,2,0:T(8,128)(2,1)} async-done(((bf16[2,1024,360]{1,2,0:T(8,128)(2,1)}), bf16[2,1024,2880]{1,2,0:T(8,128)(2,1)}) %all-gather.2.cloned.1.call-update) | async-done | bytes 11796496 | tf_op jit(solution)/shard_map/all_gather | solution.py:51
  152.4 8.8 %fusion.7 = f32[2,1024,360]{1,2,0:T(8,128)S(1)} fusion(bf16[2,1024,2880]{1,2,0:T(8,128)(2,1)} %all-gather.2.cloned.1.call-done, bf16[2,2880,360]{1,2,0:T(8,128)(2,1)} %param.9), kind=kOutput, calls=%fused_computation.37 | convolution fusion | flops 4246732800 | bytes 18892800 | tf_op jit(solution)/shard_map/erd,edf->erf/dot_general | solution.py:52
  161.3 18.4 %convolution_convert_fusion = bf16[2,1024,2880]{1,2,0:T(8,128)(2,1)} fusion(bf16[2,360,2880]{2,1,0:T(8,128)(2,1)} %param.11, f32[2,1024,360]{1,2,0:T(8,128)S(1)} %fusion.7, bf16[2,1024,2880]{1,2,0:T(8,128)(2,1)} %all-gather.2.cloned.1.call-done, bf16[2,2880,360]{1,2,0:T(8,128)(2,1)} %param.10), kind=kOutput, calls=%fused_computation.3 | convolution fusion | flops 8505262080 | bytes 34836480 | tf_op jit(solution)/shard_map/erf,efd->erd/dot_general | solution.py:57
  179.7 10.2 %copy.71 = bf16[2,4,2,1024,360]{3,4,2,1,0:T(8,128)(2,1)} copy(bf16[2,4,2,1024,360]{3,4,0,1,2:T(8,128)(2,1)} %bitcast.47) | data formatting | bytes 23592960 | tf_op jit(solution)/shard_map/transpose | solution.py:13
  190.0 26.8 %reduce-scatter.3.cloned.1.call-done = bf16[4,2,1024,360]{2,3,1,0:T(8,128)(2,1)} async-done(((bf16[8,2,1024,360]{2,3,1,0:T(8,128)(2,1)}), bf16[4,2,1024,360]{2,3,1,0:T(8,128)(2,1)}) %reduce-scatter.3.cloned.1.call-update) | async-done | bytes 5898256 | tf_op jit(solution)/shard_map/reduce_scatter | solution.py:15
  216.8 65.4 %reduce-scatter.5.cloned.1.call-done = bf16[1,2,1024,360]{2,3,1,0:T(8,128)(2,1)} async-done(((bf16[4,2,1024,360]{2,3,1,0:T(8,128)(2,1)}), bf16[1,2,1024,360]{2,3,1,0:T(8,128)(2,1)}) %reduce-scatter.5.cloned.1.call-update) | async-done | bytes 1474576 | tf_op jit(solution)/shard_map/reduce_scatter | solution.py:15
  282.2 1.8 copy.72
  284.1 1.4 copy.73
  285.5 10.1 %all-to-all-start.1 = ((bf16[2,32,32,360]{3,2,0,1:T(8,128)(2,1)}), bf16[2,32,32,360]{3,2,0,1:T(8,128)(2,1)}, u32[]{:S(2)}, u32[]{:S(2)}) async-start(bf16[2,32,32,360]{3,2,0,1:T(8,128)(2,1)} %copy.73), calls=%async_computation.3 | async-start | bytes 3145728 | tf_op jit(solution)/shard_map/all_to_all | solution.py:61
  295.6 0.1 copy.75
  295.8 39.0 %all-to-all-done.1 = bf16[2,32,32,360]{3,2,0,1:T(8,128)(2,1)} async-done(((bf16[2,32,32,360]{3,2,0,1:T(8,128)(2,1)}), bf16[2,32,32,360]{3,2,0,1:T(8,128)(2,1)}, u32[]{:S(2)}, u32[]{:S(2)}) %all-to-all-start.1) | async-done | bytes 1474592 | tf_op jit(solution)/shard_map/all_to_all | solution.py:61
  334.8 1.8 copy_convert_fusion
  336.6 14.1 %gather_fusion = f32[1024,360]{1,0:T(8,128)} fusion(f32[2,32,32,360]{3,2,1,0:T(8,128)S(1)} %copy_convert_fusion, s32[1024]{0:T(1024)S(1)} %bitcast.45), kind=kCustom, calls=%fused_computation.1 | custom fusion | bytes 2961408 | tf_op jit(solution)/shard_map/gather | solution.py:64
  350.7 1.8 gather.10
  352.5 1.0 multiply_reduce_fusion
  353.5 0.8 copy.76
  (22 shorter events, 0.5 us)
Async XLA Ops:
  6.5 20.0 %copy-start.3 = (s32[3]{0:T(128)S(1)}, s32[3]{0:T(128)}, u32[]{:S(2)}) copy-start(s32[3]{0:T(128)} %constant.60) | copy-start | bytes 40
  6.5 20.1 %copy-start.2 = (s32[3]{0:T(128)S(1)}, s32[3]{0:T(128)}, u32[]{:S(2)}) copy-start(s32[3]{0:T(128)} %constant.63) | copy-start | bytes 40
  6.5 20.2 %copy-start = (bf16[256,360]{0,1:T(8,128)(2,1)S(1)}, bf16[256,360]{0,1:T(8,128)(2,1)}, u32[]{:S(2)}) copy-start(bf16[256,360]{0,1:T(8,128)(2,1)} %param.6) | copy-start | bytes 552964
  6.5 145.9 %all-gather.2.cloned.1.call-start = ((), (), s32[]{:S(2)}) async-start(), calls=%async_computation.4 | async-start | bytes 13271040 | tf_op jit(solution)/shard_map/all_gather | solution.py:51
  89.5 127.3 %reduce-scatter.3.cloned.1.call-start = ((), (), s32[]{:S(2)}) async-start(), calls=%async_computation.5 | async-start | bytes 17694720 | tf_op jit(solution)/shard_map/reduce_scatter | solution.py:15
  190.0 92.3 %reduce-scatter.5.cloned.1.call-start = ((), (), s32[]{:S(2)}) async-start(), calls=%async_computation.6 | async-start | bytes 7372800 | tf_op jit(solution)/shard_map/reduce_scatter | solution.py:15
  284.1 11.5 %copy-start.1 = (f32[256,4]{0,1:T(4,128)S(1)}, f32[256,4]{0,1:T(4,128)}, u32[]{:S(2)}) copy-start(f32[256,4]{0,1:T(4,128)} %param.8) | copy-start | bytes 12292
  285.5 49.3 %all-to-all-start.1 = ((bf16[2,32,32,360]{3,2,0,1:T(8,128)(2,1)}), bf16[2,32,32,360]{3,2,0,1:T(8,128)(2,1)}, u32[]{:S(2)}, u32[]{:S(2)}) async-start(bf16[2,32,32,360]{3,2,0,1:T(8,128)(2,1)} %copy.73), calls=%async_computation.3 | async-start | bytes 3145728 | tf_op jit(solution)/shard_map/all_to_all | solution.py:61
Sparse Core Ops, SparseCore 0:
  89.6 62.7 all-gather.1
  190.1 26.6 reduce-scatter.2
  219.4 62.7 reduce-scatter.4
where the time goes:
time: 361 us
  waiting for transfers between devices  194 us (54%)
  blocking collectives  51.1 us (14%)
  local copies, waits for them, and re-layouts  43.5 us (12%)
  matrix products  27.3 us (8%)
  other arithmetic  21.4 us (6%)
  between operations  13.3 us (4%)
  starting transfers between devices  10.4 us (3%)
    reduce_scatter x2, waiting for transfers between devices, reduced_to_own(): pieces = lax.psum_scatter(pieces, axes[k], scatter_dimension=0, tiled=True)  92.2 us
    all_gather x1, waiting for transfers between devices, local(): shard_piece = lax.all_gather(arrived, TP, axis=2, tiled=True)  62.7 us
    all_to_all x1, blocking collectives, local(): lax.all_to_all(send_buf, 'ep', split_axis=1, concat_axis=1, tiled=True)  51.1 us
    all_to_all x1, waiting for transfers between devices, local(): lax.all_to_all(summed.astype(jnp.bfloat16), 'ep', split_axis=1, concat_ax...  39 us
    dot_general x1, matrix products, local(): jnp.einsum('erf,efd->erd', hidden, down_weight, preferred_element_type=jn...  18.4 us
    another operation x3, other arithmetic  18.2 us
    gather x2, local copies, waits for them, and re-layouts, local(): picked = returned[expert_local, owner_dev, slot_pos]  15.9 us
    unnamed x12, local copies, waits for them, and re-layouts  10.5 us
  transfers between devices with their start and end apart: 4, of which 4 were waited for; matrix products, arithmetic and copies ran while one was open for 0% of the time, Pallas kernels for 0%

commit v1 on v0

--- a/solution.py
+++ b/solution.py
@@ -48,7 +48,9 @@
     send_buf = send_buf.at[expert_local, owner_dev, slot_pos].set(tokens[token_of])
     arrived = lax.all_to_all(send_buf, "ep", split_axis=1, concat_axis=1, tiled=True)
     arrived = arrived.reshape(exp_local, ep_count * capacity, feat_width)
-    shard_piece = lax.all_gather(arrived, TP, axis=2, tiled=True)
+    shard_piece = jnp.concatenate(
+        lax.all_to_all(jnp.stack([arrived] * lax.axis_size(TP)), TP, 0, 0), axis=2
+    )
     gate_new = jnp.einsum(
         "erd,edf->erf", shard_piece, gate_weight, preferred_element_type=jnp.float32
     )

time: 361 us -> 441 us (1.22)
  blocking collectives: 51.1 us -> 187 us
  waiting for transfers between devices: 194 us -> 128 us
  local copies, waits for them, and re-layouts: 43.5 us -> 53.8 us
    all_to_all x0 -> x1, blocking collectives: none -> 136 us  [local(): lax.all_to_all(jnp.stack([arrived] * lax.axis_size(TP)), TP, 0, 0)]
    all_gather x1 -> x0, waiting for transfers between devices: 62.7 us -> none  [local(): shard_piece = lax.all_gather(arrived, TP, axis=2, tiled=True)]
    another operation x2 -> x4, local copies, waits for them, and re-layouts: 0.09 us -> 6.79 us  [the longest x2 6.7 us: local(): jnp.stack([arrived] * lax.axis_size(TP))]
  transfers between devices with their start and end apart: 4 -> 3, of which waited for: 4 -> 3; matrix products, arithmetic and copies ran while one was open for 0% -> 0% of each run, Pallas kernels for 0% -> 0%
where the time goes in v1:
time: 441 us
  blocking collectives  187 us (42%)
  waiting for transfers between devices  128 us (29%)
  local copies, waits for them, and re-layouts  53.8 us (12%)
  matrix products  27.3 us (6%)
  other arithmetic  21.4 us (5%)
  between operations  13.6 us (3%)
  starting transfers between devices  10.1 us (2%)
    all_to_all x1, blocking collectives, local(): lax.all_to_all(jnp.stack([arrived] * lax.axis_size(TP)), TP, 0, 0)  136 us
    reduce_scatter x2, waiting for transfers between devices, reduced_to_own(): pieces = lax.psum_scatter(pieces, axes[k], scatter_dimension=0, tiled=True)  89 us
    all_to_all x1, blocking collectives, local(): lax.all_to_all(send_buf, 'ep', split_axis=1, concat_axis=1, tiled=True)  51.1 us
    all_to_all x1, waiting for transfers between devices, local(): lax.all_to_all(summed.astype(jnp.bfloat16), 'ep', split_axis=1, concat_ax...  39 us
    dot_general x1, matrix products, local(): jnp.einsum('erf,efd->erd', hidden, down_weight, preferred_element_type=jn...  18.4 us
    another operation x3, other arithmetic  18.2 us
    gather x2, local copies, waits for them, and re-layouts, local(): picked = returned[expert_local, owner_dev, slot_pos]  15.9 us
    unnamed x12, local copies, waits for them, and re-layouts  10.5 us
  transfers between devices with their start and end apart: 3, of which 3 were waited for; matrix products, arithmetic and copies ran while one was open for 0% of the time, Pallas kernels for 0%

profile of v1, /device:TPU:32, one launch (start us, length us, event | category | flops | bytes accessed | tf_op | source)
XLA Modules:
  0.0 440.8 jit_solution(7967100099624271598)
XLA Ops:
  6.5 0.9 copy.64
  7.4 0.1 eq.31
  7.5 0.1 eq.27
  7.6 0.1 reshape.223
  7.8 18.0 %reduce-window.6 = s32[64,8,128]{2,1,0:T(8,128)S(1)} reduce-window(s32[64,8,128]{2,1,0:T(8,128)S(1)} %fusion.6, s32[]{:T(128)} %constant.47.clone.1), window={size=1x1x128 pad=0_0x0_0x127_0}, to_apply=%region_0.0 | reduce-window | flops 8323072 | bytes 524292 | tf_op jit(solution)/shard_map/reduce-window
  25.8 0.1 slice.13
  26.0 0.1 copy.67
  26.2 0.1 broadcast_add_fusion
  26.7 0.2 copy.69
  26.9 9.4 %scatter_custom_fusion = bf16[2048,360]{1,0:T(8,128)(2,1)S(1)} fusion(s32[1024]{0:T(1024)S(1)} %get-tuple-element.10, bf16[256,360]{1,0:T(8,128)(2,1)S(1)} %copy.69, s32[1024]{0:T(1024)S(1)} %get-tuple-element.9, bf16[]{:T(256)} %constant.46.clone.1), kind=kCustom, calls=%fused_computation.7 | custom fusion | bytes 1474562
  36.3 0.3 copy.70
  36.6 51.1 %all_to_all.15 = bf16[2,32,32,360]{3,2,0,1:T(8,128)(2,1)S(1)} all-to-all(bf16[2,32,32,360]{3,2,0,1:T(8,128)(2,1)S(1)} %copy.70), channel_id=1, replica_groups=mesh['ep'=32,'tp_0'=4,'tp_1'=2] {'ep'}, dimensions={1} | all-to-all | bytes 2949120 | tf_op jit(solution)/shard_map/all_to_all | solution.py:49
  87.6 0.2 copy.71
  87.8 0.7 copy.72
  88.6 6.0 %stack.3 = bf16[8,2,1024,360]{2,3,1,0:T(8,128)(2,1)} broadcast(bf16[2,1024,360]{1,2,0:T(8,128)(2,1)S(1)} %copy.72), dimensions={1,2,3} | broadcast | bytes 13271040 | tf_op jit(solution)/shard_map/stack | solution.py:52
  94.5 135.6 %all_to_all.16 = bf16[8,2,1024,360]{2,3,1,0:T(8,128)(2,1)S(1)} all-to-all(bf16[8,2,1024,360]{2,3,1,0:T(8,128)(2,1)} %stack.3), channel_id=1, replica_groups=mesh['ep'=32,'tp_0'=4,'tp_1'=2] {'tp_0','tp_1'}, dimensions={0} | all-to-all | bytes 23592960 | tf_op jit(solution)/shard_map/all_to_all | solution.py:52
  230.1 5.1 %copy.73 = bf16[2,1024,8,360]{1,3,2,0:T(8,128)(2,1)} copy(bf16[2,1024,8,360]{1,3,0,2:T(8,128)(2,1)S(1)} %bitcast.49) | data formatting | bytes 23592960 | tf_op jit(solution)/shard_map/reshape | solution.py:51
  235.2 8.8 %fusion.7 = f32[2,1024,360]{1,2,0:T(8,128)S(1)} fusion(bf16[2,1024,2880]{1,2,0:T(8,128)(2,1)} %bitcast.50, bf16[2,2880,360]{1,2,0:T(8,128)(2,1)} %param.9), kind=kOutput, calls=%fused_computation.37 | convolution fusion | flops 4246732800 | bytes 18892800 | tf_op jit(solution)/shard_map/erd,edf->erf/dot_general | solution.py:54
  244.1 18.4 %convolution_convert_fusion = bf16[2,1024,2880]{1,2,0:T(8,128)(2,1)} fusion(bf16[2,360,2880]{2,1,0:T(8,128)(2,1)} %param.11, f32[2,1024,360]{1,2,0:T(8,128)S(1)} %fusion.7, bf16[2,1024,2880]{1,2,0:T(8,128)(2,1)} %bitcast.51, bf16[2,2880,360]{1,2,0:T(8,128)(2,1)} %param.10), kind=kOutput, calls=%fused_computation.3 | convolution fusion | flops 8505262080 | bytes 34836480 | tf_op jit(solution)/shard_map/erf,efd->erd/dot_general | solution.py:59
  262.5 10.2 %copy.75 = bf16[2,4,2,1024,360]{3,4,2,1,0:T(8,128)(2,1)} copy(bf16[2,4,2,1024,360]{3,4,0,1,2:T(8,128)(2,1)} %bitcast.52) | data formatting | bytes 23592960 | tf_op jit(solution)/shard_map/transpose | solution.py:13
  272.8 19.8 %reduce-scatter.3.cloned.1.call-done = bf16[4,2,1024,360]{2,3,1,0:T(8,128)(2,1)} async-done(((bf16[8,2,1024,360]{2,3,1,0:T(8,128)(2,1)}), bf16[4,2,1024,360]{2,3,1,0:T(8,128)(2,1)}) %reduce-scatter.3.cloned.1.call-update) | async-done | bytes 5898256 | tf_op jit(solution)/shard_map/reduce_scatter | solution.py:15
  292.7 69.1 %reduce-scatter.5.cloned.1.call-done = bf16[1,2,1024,360]{2,3,1,0:T(8,128)(2,1)} async-done(((bf16[4,2,1024,360]{2,3,1,0:T(8,128)(2,1)}), bf16[1,2,1024,360]{2,3,1,0:T(8,128)(2,1)}) %reduce-scatter.5.cloned.1.call-update) | async-done | bytes 1474576 | tf_op jit(solution)/shard_map/reduce_scatter | solution.py:15
  361.8 1.9 copy.76
  363.7 1.5 copy.77
  365.2 10.1 %all-to-all-start.2 = ((bf16[2,32,32,360]{3,2,0,1:T(8,128)(2,1)}), bf16[2,32,32,360]{3,2,0,1:T(8,128)(2,1)}, u32[]{:S(2)}, u32[]{:S(2)}) async-start(bf16[2,32,32,360]{3,2,0,1:T(8,128)(2,1)} %copy.77), calls=%async_computation.4 | async-start | bytes 3145728 | tf_op jit(solution)/shard_map/all_to_all | solution.py:63
  375.3 0.1 copy.79
  375.4 39.0 %all-to-all-done.2 = bf16[2,32,32,360]{3,2,0,1:T(8,128)(2,1)} async-done(((bf16[2,32,32,360]{3,2,0,1:T(8,128)(2,1)}), bf16[2,32,32,360]{3,2,0,1:T(8,128)(2,1)}, u32[]{:S(2)}, u32[]{:S(2)}) %all-to-all-start.2) | async-done | bytes 1474592 | tf_op jit(solution)/shard_map/all_to_all | solution.py:63
  414.4 1.8 copy_convert_fusion
  416.2 14.1 %gather_fusion = f32[1024,360]{1,0:T(8,128)} fusion(f32[2,32,32,360]{3,2,1,0:T(8,128)S(1)} %copy_convert_fusion, s32[1024]{0:T(1024)S(1)} %bitcast.47), kind=kCustom, calls=%fused_computation.1 | custom fusion | bytes 2961408 | tf_op jit(solution)/shard_map/gather | solution.py:66
  430.4 1.8 gather.10
  432.1 1.0 multiply_reduce_fusion
  433.2 0.8 copy.80
  (22 shorter events, 0.6 us)
Async XLA Ops:
  6.5 20.0 %copy-start.3 = (s32[3]{0:T(128)S(1)}, s32[3]{0:T(128)}, u32[]{:S(2)}) copy-start(s32[3]{0:T(128)} %constant.60) | copy-start | bytes 40
  6.5 20.1 %copy-start.2 = (s32[3]{0:T(128)S(1)}, s32[3]{0:T(128)}, u32[]{:S(2)}) copy-start(s32[3]{0:T(128)} %constant.63) | copy-start | bytes 40
  6.5 20.2 %copy-start = (bf16[256,360]{0,1:T(8,128)(2,1)S(1)}, bf16[256,360]{0,1:T(8,128)(2,1)}, u32[]{:S(2)}) copy-start(bf16[256,360]{0,1:T(8,128)(2,1)} %param.6) | copy-start | bytes 552964
  6.5 286.1 %reduce-scatter.3.cloned.1.call-start = ((), (), s32[]{:S(2)}) async-start(), calls=%async_computation.5 | async-start | bytes 17694720 | tf_op jit(solution)/shard_map/reduce_scatter | solution.py:15
  272.8 89.0 %reduce-scatter.5.cloned.1.call-start = ((), (), s32[]{:S(2)}) async-start(), calls=%async_computation.6 | async-start | bytes 7372800 | tf_op jit(solution)/shard_map/reduce_scatter | solution.py:15
  363.7 11.6 %copy-start.1 = (f32[256,4]{0,1:T(4,128)S(1)}, f32[256,4]{0,1:T(4,128)}, u32[]{:S(2)}) copy-start(f32[256,4]{0,1:T(4,128)} %param.8) | copy-start | bytes 12292
  365.2 49.2 %all-to-all-start.2 = ((bf16[2,32,32,360]{3,2,0,1:T(8,128)(2,1)}), bf16[2,32,32,360]{3,2,0,1:T(8,128)(2,1)}, u32[]{:S(2)}, u32[]{:S(2)}) async-start(bf16[2,32,32,360]{3,2,0,1:T(8,128)(2,1)} %copy.77), calls=%async_computation.4 | async-start | bytes 3145728 | tf_op jit(solution)/shard_map/all_to_all | solution.py:63
Sparse Core Ops, SparseCore 0:
  272.9 19.7 reduce-scatter.2
  295.2 66.5 reduce-scatter.4
